TPU v7x, 512 devices: a 4x2x32 block of a 4x8x32 slice. The times are simulated.
512 devices in a mesh: grp: 2 (over y), row: 32 (over z), col: 4 (over x), sub: 2 (over core).
Axes of the slice: x: 4, y: 2, z: 32, core: 2. Of those that a mesh axis runs over, the one named last changes fastest.
The devices are a block of a 4x8x32 slice.
Arguments:
- pair: bfloat16 [768, 384, 128], P(('grp', 'row'), 'col'), parts along dimension 0, may hold values from -6 to 6
- length: int32 [2], P('grp'), parts along dimension 0, may hold values from 192 to 384
- chain: int32 [768], P('grp'), parts along dimension 0, may hold values from 0 to 3, never falling along the last dimension, each value on 1 to 192 neighbouring positions
- att_proj: bfloat16 [128, 4, 128], P(None, None, 'sub'), may hold values from -0.5 to 0.5
- att_bias: bfloat16 [128, 4], P(None, 'sub')
- chain_bias: float32 [4], P('sub'), may hold values from -2 to 2
- att_out: bfloat16 [128, 128], P('sub'), may hold values from -0.5 to 0.5
- mult_in: bfloat16 [128, 512], replicated, may hold values from -0.5 to 0.5
- mult_gate: bfloat16 [128, 128], replicated, may hold values from -0.5 to 0.5
- mult_out: bfloat16 [128, 128], replicated, may hold values from -0.5 to 0.5
- trans_up: bfloat16 [128, 512], replicated, may hold values from -0.5 to 0.5
- trans_down: bfloat16 [512, 128], replicated, may hold values from -0.25 to 0.25
Outputs:
- pair_out: bfloat16 [768, 384, 128], P(('grp', 'row'), ('col', 'sub')), parts along dimension 0
There are 2 independent parts, one for each index of `grp`. A program takes and returns all parts, laid end to end along the dimension named above; an argument that names none is the same for every part. Nothing has to cross between parts.
Inputs may be any that keep to these rules, and one draw needn't show every extreme that they name: chain numbers never fall along the residues; each chain has 1 to 192 residues.
All inputs are finite; a program needn't handle non-finite values.
Results may differ from a plain program's by a relative error of at most 0.012.
The roundings to bfloat16 on the way count: a program that leaves them out, or rounds other values in their place, can miss the bound.
Values may be sent and summed in bfloat16 or wider, within the bound.
A program may use at most 64 MiB of HBM per device.

v0:
```python
import jax
import jax.numpy as jnp
from jax import lax
from jax.sharding import PartitionSpec as P


def sent_together(arrays, axis, dim, along):
    ends, at = ([], 0)
    for a in arrays[:-1]:
        at += a.shape[along]
        ends.append(at)
    both = jnp.concatenate(arrays, axis=along)
    return tuple(jnp.split(lax.all_gather(both, axis, axis=dim, tiled=True), ends, axis=along))


def joined_along(blocks, dim):
    shape = list(blocks.shape[1:])
    shape[dim] *= blocks.shape[0]
    return jnp.moveaxis(blocks, 0, dim).reshape(shape)


def copy_for_each(shard, axis):
    devices = lax.axis_size(axis)
    return lax.all_to_all(
        jnp.broadcast_to(shard[None], (devices, *shard.shape)), axis, 0, 0, tiled=True
    )


def collect(shard, axis, dim):
    return joined_along(copy_for_each(shard, axis), dim)


def cut_along(shard, dim, devices):
    before, after = (shard.shape[:dim], shard.shape[dim + 1 :])
    return jnp.moveaxis(shard.reshape(*before, devices, -1, *after), dim, 0)


def sum_at_owner(shard, axis, dim):
    devices = lax.axis_size(axis)
    blocks = lax.all_to_all(cut_along(shard, dim, devices), axis, 0, 0, tiled=True)
    return jnp.sum(blocks.astype(jnp.float32), axis=0)


def norm(value):
    mean = jnp.mean(value, axis=-1, keepdims=True)
    centred = value - mean
    variance = jnp.mean(centred * centred, axis=-1, keepdims=True)
    return centred * lax.rsqrt(variance + 1e-05)


def local(
    pair,
    length,
    chain,
    att_proj,
    att_bias,
    chain_bias,
    att_out,
    mult_in,
    mult_gate,
    mult_out,
    trans_up,
    trans_down,
):
    rows, cols, width = pair.shape
    row_count = lax.axis_size("row")
    sub_count = lax.axis_size("sub")
    row_index = lax.axis_index("row")
    col_index = lax.axis_index("col")
    sub_index = lax.axis_index("sub")
    total = rows * row_count
    half = cols // sub_count
    heads_here = att_bias.shape[1]
    spread = att_out.shape[0]
    head_dim = spread // heads_here
    mult_width = mult_out.shape[0]
    valid = (jnp.arange(total) < length[0]).astype(jnp.float32)
    normed = norm(pair.astype(jnp.float32)).astype(jnp.bfloat16)
    flat = normed.reshape(rows * cols, width)
    projected = jnp.dot(
        flat, att_proj.reshape(width, 4 * spread), preferred_element_type=jnp.float32
    ).reshape(rows, cols, 4, spread)
    query = (projected[:, :, 0] * head_dim ** (-0.5)).astype(jnp.bfloat16)
    keys = projected[:, :, 1].astype(jnp.bfloat16)
    values = projected[:, :, 2].astype(jnp.bfloat16)
    gating = jax.nn.sigmoid(projected[:, :, 3])
    bias_local = (
        jnp.dot(flat, att_bias, preferred_element_type=jnp.float32)
        .reshape(rows, cols, heads_here)
        .transpose(2, 0, 1)
    )
    keys_all, values_all = sent_together((keys, values), "col", 1, 0)
    column_bias = collect(bias_local, "row", 1)
    bias_here = lax.all_to_all(column_bias, "col", split_axis=1, concat_axis=2, tiled=True)
    chain_here = lax.dynamic_slice_in_dim(chain, col_index * cols, cols, 0)
    same = (chain_here[:, None] == chain[None, :]).astype(jnp.float32)
    bias_here = (
        bias_here
        + chain_bias[:, None, None] * same[None]
        + (valid[None, None, :] - 1.0) * 1000000000.0
    )

    def attend(block):
        block_query, block_keys, block_values = block
        scores = (
            jnp.einsum(
                "ajhd,akhd->ahjk", block_query, block_keys, preferred_element_type=jnp.float32
            )
            + bias_here[None]
        )
        weights = jax.nn.softmax(scores, axis=-1).astype(jnp.bfloat16)
        return jnp.einsum(
            "ahjk,akhd->ajhd", weights, block_values, preferred_element_type=jnp.float32
        )

    attended = lax.map(
        attend,
        (
            query.reshape(rows // 2, 2, cols, heads_here, head_dim),
            keys_all.reshape(rows // 2, 2, total, heads_here, head_dim),
            values_all.reshape(rows // 2, 2, total, heads_here, head_dim),
        ),
    )
    attended = (attended.reshape(rows, cols, spread) * gating).astype(jnp.bfloat16)
    update = jnp.dot(
        attended.reshape(rows * cols, spread), att_out, preferred_element_type=jnp.float32
    ).reshape(rows, cols, width)
    update_half = sum_at_owner(update.astype(jnp.bfloat16), "sub", 1)
    pair_half = lax.dynamic_slice_in_dim(pair, sub_index * half, half, 1).astype(jnp.float32)
    first = pair_half + update_half
    mixed = norm(first).astype(jnp.bfloat16)
    mixed_flat = mixed.reshape(rows * half, width)
    quad = jnp.dot(mixed_flat, mult_in, preferred_element_type=jnp.float32).reshape(
        rows, half, 4, mult_width
    )
    row_valid = lax.dynamic_slice_in_dim(valid, row_index * rows, rows, 0)
    col_valid = lax.dynamic_slice_in_dim(valid, col_index * cols + sub_index * half, half, 0)
    outer = row_valid[:, None, None] * col_valid[None, :, None]
    left = (outer * jax.nn.sigmoid(quad[:, :, 1]) * quad[:, :, 0]).astype(jnp.bfloat16)
    right = (outer * jax.nn.sigmoid(quad[:, :, 3]) * quad[:, :, 2]).astype(jnp.bfloat16)
    gate_out = jax.nn.sigmoid(jnp.dot(mixed_flat, mult_gate, preferred_element_type=jnp.float32))
    partial_value = jnp.einsum(
        "ikc,jkc->ijc",
        left,
        lax.all_gather(right, "row", axis=0, tiled=True),
        preferred_element_type=jnp.float32,
    )
    tri = sum_at_owner(partial_value.astype(jnp.bfloat16), ("col", "sub"), 1)
    tri_normed = norm(tri).astype(jnp.bfloat16).reshape(rows * half, mult_width)
    second = first + (
        gate_out * jnp.dot(tri_normed, mult_out, preferred_element_type=jnp.float32)
    ).reshape(rows, half, width)
    last_normed = norm(second).astype(jnp.bfloat16).reshape(rows * half, width)
    hidden = jax.nn.relu(jnp.dot(last_normed, trans_up, preferred_element_type=jnp.float32)).astype(
        jnp.bfloat16
    )
    result = second + jnp.dot(hidden, trans_down, preferred_element_type=jnp.float32).reshape(
        rows, half, width
    )
    return result.astype(jnp.bfloat16)


def solution(mesh):
    placed = (
        P(("grp", "row"), "col", None),
        P("grp"),
        P("grp"),
        P(None, None, "sub"),
        P(None, "sub"),
        P("sub"),
        P("sub", None),
        P(),
        P(),
        P(),
        P(),
        P(),
    )
    return jax.shard_map(
        local,
        mesh=mesh,
        in_specs=placed,
        out_specs=P(("grp", "row"), ("col", "sub"), None),
        check_vma=False,
    )
```

profile of v0, /device:TPU:33, one launch (start us, length us, event | category | flops | bytes accessed | tf_op | source)
XLA Modules:
  0.0 350.1 jit_solution(3556476479673316180)
XLA Ops:
  6.6 1.2 convert_reduce_fusion.2
  7.8 1.4 fusion.28
  9.2 1.4 convolution_bitcast_fusion.1
  11.5 46.3 %all-to-all-start = ((f32[32,2,12,96]{3,1,2,0:T(2,128)}), f32[32,2,12,96]{3,1,2,0:T(2,128)}, u32[]{:S(2)}, u32[]{:S(2)}) async-start(f32[32,2,12,96]{3,1,2,0:T(2,128)} %broadcast_in_dim.8), calls=%async_computation | async-start | bytes 786432 | tf_op jit(solution)/shard_map/all_to_all | solution.py:24
  61.5 47.7 %all-to-all-done = f32[32,2,12,96]{3,1,2,0:T(2,128)} async-done(((f32[32,2,12,96]{3,1,2,0:T(2,128)}), f32[32,2,12,96]{3,1,2,0:T(2,128)}, u32[]{:S(2)}, u32[]{:S(2)}) %all-to-all-start) | async-done | bytes 294944 | tf_op jit(solution)/shard_map/all_to_all | solution.py:24
  109.2 4.3 %all-to-all-start.1 = ((f32[2,384,96]{2,0,1:T(2,128)}), f32[2,384,96]{2,0,1:T(2,128)S(1)}, u32[]{:S(2)}, u32[]{:S(2)}) async-start(f32[2,384,96]{2,0,1:T(2,128)} %bitcast.19), calls=%async_computation.1 | async-start | bytes 786432 | tf_op jit(solution)/shard_map/all_to_all | solution.py:94
  113.5 3.7 %fusion.78 = (bf16[12,384,64]{2,0,1:T(8,128)(2,1)S(1)}, bf16[12,384,64]{2,0,1:T(8,128)(2,1)}) fusion(bf16[24,384,64]{2,0,1:T(8,128)(2,1)} %all-gather.3.cloned.1.call-done), kind=kLoop, calls=%fused_computation.111 | loop fusion | bytes 2359296 | tf_op jit(solution)/shard_map/split | solution.py:13
  117.3 2.6 copy.91
  119.9 1.5 copy.92
  122.4 14.8 %while.10 = (s32[]{:T(128)}, f32[6,2,96,2,32]{2,4,3,1,0:T(8,128)S(1)}, bf16[6,2,384,2,32]{2,4,3,1,0:T(8,128)(2,1)}, bf16[6,2,96,2,32]{2,4,3,1,0:T(8,128)(2,1)S(1...) while((s32[]{:T(128)}, f32[6,2,96,2,32]{2,4,3,1,0:T(8,128)S(1)}, ...), condition=%wide.region_5.6_spmd, body=%wide.region_2.5_spmd.sunk | while | flops 29344896 | bytes 2792013 | solution.py:116
  123.2 1.7 fusion.106
  125.6 1.7 fusion.106
  128.1 1.7 fusion.106
  130.6 1.7 fusion.106
  133.0 1.7 fusion.106
  135.5 1.7 fusion.106
  137.2 1.3 convolution_convert_fusion.1
  138.6 6.7 %all_to_all.33 = bf16[2,12,48,128]{3,2,1,0:T(8,128)(2,1)S(1)} all-to-all(bf16[2,12,48,128]{3,2,1,0:T(8,128)(2,1)S(1)} %bitcast.193), channel_id=1, replica_groups=mesh['grp'=2,'row'=32,'col'=4,'sub'=2] {'sub'}, dimensions={0} | all-to-all | bytes 589824 | tf_op jit(solution)/shard_map/all_to_all | solution.py:40
  148.3 121.5 %all-gather.5.cloned.1.call-done = bf16[384,48,128]{2,1,0:T(8,128)(2,1)} async-done(((bf16[12,48,128]{2,1,0:T(8,128)(2,1)}), bf16[384,48,128]{2,1,0:T(8,128)(2,1)}) %all-gather.5.cloned.1.call-update) | async-done | bytes 4718608 | tf_op jit(solution)/shard_map/all_gather | solution.py:145
  269.9 17.9 %copy.81 = bf16[384,48,128]{1,0,2:T(8,128)(2,1)} copy(bf16[384,48,128]{2,1,0:T(8,128)(2,1)} %all-gather.5.cloned.1.call-done) | data formatting | bytes 9437184 | tf_op jit(solution)/shard_map/all_gather | solution.py:145
  287.8 9.0 %fusion.20 = bf16[12,384,128]{1,0,2:T(8,128)(2,1)S(1)} fusion(bf16[384,48,128]{1,0,2:T(8,128)(2,1)} %copy.81, bf16[12,48,128]{1,0,2:T(8,128)(2,1)S(1)} %copy.82), kind=kOutput, calls=%fused_computation.21 | convolution fusion | flops 57212928 | bytes 6045696 | tf_op jit(solution)/shard_map/ikc,jkc->ijc/dot_general | solution.py:142
  296.8 1.3 copy.83
  299.2 24.6 %all-to-all-start.3 = ((bf16[8,12,48,128]{3,2,1,0:T(8,128)(2,1)}), bf16[8,12,48,128]{3,2,1,0:T(8,128)(2,1)S(1)}, u32[]{:S(2)}, u32[]{:S(2)}) async-start(bf16[8,12,48,128]{3,2,1,0:T(8,128)(2,1)} %copy.84), calls=%async_computation.3 | async-start | bytes 2359296 | tf_op jit(solution)/shard_map/all_to_all | solution.py:40
  324.1 16.1 %all-to-all-done.3 = bf16[8,12,48,128]{3,2,1,0:T(8,128)(2,1)S(1)} async-done(((bf16[8,12,48,128]{3,2,1,0:T(8,128)(2,1)}), bf16[8,12,48,128]{3,2,1,0:T(8,128)(2,1)S(1)}, u32[]{:S(2)}, u32[]{:S(2)}) %all-to-all-start.3) | async-done | bytes 1179680 | tf_op jit(solution)/shard_map/all_to_all | solution.py:40
  (93 shorter events, 16.6 us)
Async XLA Ops:
  6.5 335.5 %copy-start = (bf16[512,128]{1,0:T(8,128)(2,1)S(1)}, bf16[512,128]{1,0:T(8,128)(2,1)}, u32[]{:S(2)}) copy-start(bf16[512,128]{1,0:T(8,128)(2,1)} %param.25) | copy-start | bytes 393220
  6.6 51.4 %copy-start.1 = (bf16[12,96,128]{2,1,0:T(8,128)(2,1)S(1)}, bf16[12,96,128]{2,1,0:T(8,128)(2,1)}, u32[]{:S(2)}) copy-start(bf16[12,96,128]{2,1,0:T(8,128)(2,1)} %param.14) | copy-start | bytes 884740
  6.6 51.4 %copy-start.6 = (bf16[128,4,64]{0,2,1:T(8,128)(2,1)S(1)}, bf16[128,4,64]{0,2,1:T(8,128)(2,1)}, u32[]{:S(2)}) copy-start(bf16[128,4,64]{0,2,1:T(8,128)(2,1)} %param.17) | copy-start | bytes 196612
  11.5 97.7 %all-to-all-start = ((f32[32,2,12,96]{3,1,2,0:T(2,128)}), f32[32,2,12,96]{3,1,2,0:T(2,128)}, u32[]{:S(2)}, u32[]{:S(2)}) async-start(f32[32,2,12,96]{3,1,2,0:T(2,128)} %broadcast_in_dim.8), calls=%async_computation | async-start | bytes 786432 | tf_op jit(solution)/shard_map/all_to_all | solution.py:24
  57.9 55.7 %all-gather.3.cloned.1.call-start = ((), (), s32[]{:S(2)}) async-start(), calls=%async_computation.4 | async-start | bytes 2949120 | tf_op jit(solution)/shard_map/all_gather | solution.py:13
  58.8 2.6 copy-start.2
  58.9 2.1 copy-start.5
  58.9 2.3 copy-start.8
  109.2 12.2 %all-to-all-start.1 = ((f32[2,384,96]{2,0,1:T(2,128)}), f32[2,384,96]{2,0,1:T(2,128)S(1)}, u32[]{:S(2)}, u32[]{:S(2)}) async-start(f32[2,384,96]{2,0,1:T(2,128)} %bitcast.19), calls=%async_computation.1 | async-start | bytes 786432 | tf_op jit(solution)/shard_map/all_to_all | solution.py:94
  113.5 156.3 %all-gather.5.cloned.1.call-start = ((), (), s32[]{:S(2)}) async-start(), calls=%async_computation.5 | async-start | bytes 4866048 | tf_op jit(solution)/shard_map/all_gather | solution.py:145
  119.9 2.0 copy-start.9
  121.4 1.0 copy-start.13
  122.4 14.8 %copy-start.12 = (bf16[64,128]{1,0:T(8,128)(2,1)S(1)}, bf16[64,128]{1,0:T(8,128)(2,1)}, u32[]{:S(2)}) copy-start(bf16[64,128]{1,0:T(8,128)(2,1)} %param.20) | copy-start | bytes 49156
  146.0 0.7 copy-start.3
  299.2 24.6 %copy-start.4 = (bf16[12,48,128]{2,1,0:T(8,128)(2,1)S(1)}, bf16[12,48,128]{2,1,0:T(8,128)(2,1)}, u32[]{:S(2)}) copy-start(bf16[12,48,128]{2,1,0:T(8,128)(2,1)} %copy-done.3) | copy-start | bytes 442372
  299.2 24.6 %copy-start.11 = (bf16[128,128]{1,0:T(8,128)(2,1)S(1)}, bf16[128,128]{1,0:T(8,128)(2,1)}, u32[]{:S(2)}) copy-start(bf16[128,128]{1,0:T(8,128)(2,1)} %param.22) | copy-start | bytes 98308
  299.2 41.0 %all-to-all-start.3 = ((bf16[8,12,48,128]{3,2,1,0:T(8,128)(2,1)}), bf16[8,12,48,128]{3,2,1,0:T(8,128)(2,1)S(1)}, u32[]{:S(2)}, u32[]{:S(2)}) async-start(bf16[8,12,48,128]{3,2,1,0:T(8,128)(2,1)} %copy.84), calls=%async_computation.3 | async-start | bytes 2359296 | tf_op jit(solution)/shard_map/all_to_all | solution.py:40
  323.9 17.3 %copy-start.7 = (bf16[128,128]{1,0:T(8,128)(2,1)S(1)}, bf16[128,128]{1,0:T(8,128)(2,1)}, u32[]{:S(2)}) copy-start(bf16[128,128]{1,0:T(8,128)(2,1)} %param.23) | copy-start | bytes 98308
  340.8 1.2 copy-start.10
Sparse Core Ops, SparseCore 0:
  60.8 50.1 all-gather.2
  148.0 121.8 all-gather.4
where the time goes:
time: 351 us; the launch traced here: 350 us
  waiting for transfers between devices  185 us (53%)
  starting transfers between devices  75.3 us (21%)
  local copies, waits for them, and re-layouts  32.7 us (9%)
  matrix products  28.6 us (8%)
  between operations  14.5 us (4%)
  other arithmetic  6.71 us (2%)
  blocking collectives  6.71 us (2%)
    all_gather x1, waiting for transfers between devices, local(): lax.all_gather(right, 'row', axis=0, tiled=True)  122 us
    all_to_all x1, waiting for transfers between devices, copy_for_each(): lax.all_to_all(jnp.broadcast_to(shard[None], (devices, *shard.shape)), ax...  47.7 us
    all_to_all x1, starting transfers between devices, copy_for_each(): lax.all_to_all(jnp.broadcast_to(shard[None], (devices, *shard.shape)), ax...  46.3 us
    all_to_all x1, starting transfers between devices, sum_at_owner(): lax.all_to_all(cut_along(shard, dim, devices), axis, 0, 0, tiled=True)  24.6 us
    all_gather x1, local copies, waits for them, and re-layouts, local(): lax.all_gather(right, 'row', axis=0, tiled=True)  17.9 us
    all_to_all x1, waiting for transfers between devices, sum_at_owner(): lax.all_to_all(cut_along(shard, dim, devices), axis, 0, 0, tiled=True)  16.1 us
    dot_general x6, matrix products, attend(): jnp.einsum('ahjk,akhd->ajhd', weights, block_values, preferred_element_ty...  10.1 us
    dot_general x1, matrix products, local(): jnp.einsum('ikc,jkc->ijc', left, lax.all_gather(right, 'row', axis=0, til...  9.04 us
  transfers between devices with their start and end apart: 5, of which 3 were waited for; matrix products, arithmetic and copies ran while one was open for 3% of the time, Pallas kernels for 0%

commit v1 on v0

--- a/solution.py
+++ b/solution.py
@@ -1,7 +1,19 @@
+import functools
 import jax
 import jax.numpy as jnp
 from jax import lax
 from jax.sharding import PartitionSpec as P
+from jax.lax import all_to_all, axis_size
+
+
+def touch_orders(state, d_out):
+    return jnp.concatenate(
+        all_to_all(jnp.stack([state for _ in range(axis_size("row"))], axis=0), "row", 0, 0),
+        axis=d_out,
+    )
+
+
+perform_pieces_all = functools.partial(touch_orders, d_out=0)
 
 
 def sent_together(arrays, axis, dim, along):
@@ -140,10 +152,7 @@
     right = (outer * jax.nn.sigmoid(quad[:, :, 3]) * quad[:, :, 2]).astype(jnp.bfloat16)
     gate_out = jax.nn.sigmoid(jnp.dot(mixed_flat, mult_gate, preferred_element_type=jnp.float32))
     partial_value = jnp.einsum(
-        "ikc,jkc->ijc",
-        left,
-        lax.all_gather(right, "row", axis=0, tiled=True),
-        preferred_element_type=jnp.float32,
+        "ikc,jkc->ijc", left, perform_pieces_all(right), preferred_element_type=jnp.float32
     )
     tri = sum_at_owner(partial_value.astype(jnp.bfloat16), ("col", "sub"), 1)
     tri_normed = norm(tri).astype(jnp.bfloat16).reshape(rows * half, mult_width)

time: 351 us -> 635 us (1.81); the launches traced: 350 us -> 623 us
  waiting for transfers between devices: 185 us -> 470 us
  local copies, waits for them, and re-layouts: 32.7 us -> 25.6 us
    all_to_all x0 -> x1, waiting for transfers between devices: none -> 406 us  [touch_orders(): all_to_all(jnp.stack([state for _ in range(axis_size('row'))], axis=0), '...]
    all_gather x1 -> x0, waiting for transfers between devices: 122 us -> none  [local(): lax.all_gather(right, 'row', axis=0, tiled=True)]
    all_to_all x0 -> x1, starting transfers between devices: none -> 22.9 us  [touch_orders(): all_to_all(jnp.stack([state for _ in range(axis_size('row'))], axis=0), '...]
    all_to_all x1, starting transfers between devices: 24.6 us -> 4.51 us  [sum_at_owner(): lax.all_to_all(cut_along(shard, dim, devices), axis, 0, 0, tiled=True)]
    all_gather x1 -> x0, local copies, waits for them, and re-layouts: 17.9 us -> none  [local(): lax.all_gather(right, 'row', axis=0, tiled=True)]
    reshape x0 -> x1, local copies, waits for them, and re-layouts: none -> 7.59 us  [touch_orders(): jnp.concatenate(all_to_all(jnp.stack([state for _ in range(axis_size('row...]
  transfers between devices with their start and end apart: 5 -> 5, of which waited for: 3 -> 3; matrix products, arithmetic and copies ran while one was open for 3% -> 2% of each run, Pallas kernels for 0% -> 0%
where the time goes in v1:
time: 635 us; the launch traced here: 623 us
  waiting for transfers between devices  470 us (74%)
  starting transfers between devices  78.1 us (12%)
  local copies, waits for them, and re-layouts  25.6 us (4%)
  matrix products  22.8 us (4%)
  between operations  14.5 us (2%)
  blocking collectives  6.65 us (1%)
    all_to_all x1, waiting for transfers between devices, touch_orders(): all_to_all(jnp.stack([state for _ in range(axis_size('row'))], axis=0), '...  406 us
    all_to_all x1, waiting for transfers between devices, copy_for_each(): lax.all_to_all(jnp.broadcast_to(shard[None], (devices, *shard.shape)), ax...  47.7 us
    all_to_all x1, starting transfers between devices, copy_for_each(): lax.all_to_all(jnp.broadcast_to(shard[None], (devices, *shard.shape)), ax...  46.3 us
    all_to_all x1, starting transfers between devices, touch_orders(): all_to_all(jnp.stack([state for _ in range(axis_size('row'))], axis=0), '...  22.9 us
    all_to_all x1, waiting for transfers between devices, sum_at_owner(): lax.all_to_all(cut_along(shard, dim, devices), axis, 0, 0, tiled=True)  16.2 us
  transfers between devices with their start and end apart: 5, of which 3 were waited for; matrix products, arithmetic and copies ran while one was open for 2% of the time, Pallas kernels for 0%

profile of v1, /device:TPU:33, one launch (start us, length us, event | category | flops | bytes accessed | tf_op | source)
XLA Modules:
  0.0 623.4 jit_solution(7619828534249152553)
XLA Ops:
  7.8 1.4 fusion.28
  9.2 1.4 convolution_bitcast_fusion.1
  11.5 46.3 %all-to-all-start = ((f32[32,2,12,96]{3,1,2,0:T(2,128)}), f32[32,2,12,96]{3,1,2,0:T(2,128)}, u32[]{:S(2)}, u32[]{:S(2)}) async-start(f32[32,2,12,96]{3,1,2,0:T(2,128)} %broadcast_in_dim.8), calls=%async_computation | async-start | bytes 786432 | tf_op jit(solution)/shard_map/all_to_all | solution.py:36
  61.5 47.7 %all-to-all-done = f32[32,2,12,96]{3,1,2,0:T(2,128)} async-done(((f32[32,2,12,96]{3,1,2,0:T(2,128)}), f32[32,2,12,96]{3,1,2,0:T(2,128)}, u32[]{:S(2)}, u32[]{:S(2)}) %all-to-all-start) | async-done | bytes 294944 | tf_op jit(solution)/shard_map/all_to_all | solution.py:36
  109.2 4.3 all-to-all-start.1
  113.5 3.7 fusion.78
  117.3 2.6 copy.91
  119.9 1.5 copy.92
  122.4 14.8 %while.10 = (s32[]{:T(128)}, f32[6,2,96,2,32]{2,4,3,1,0:T(8,128)S(1)}, bf16[6,2,384,2,32]{2,4,3,1,0:T(8,128)(2,1)}, bf16[6,2,96,2,32]{2,4,3,1,0:T(8,128)(2,1)S(1...) while((s32[]{:T(128)}, f32[6,2,96,2,32]{2,4,3,1,0:T(8,128)S(1)}, ...), condition=%wide.region_5.6_spmd, body=%wide.region_2.5_spmd.sunk | while | flops 29344896 | bytes 2792013 | solution.py:128
  123.2 1.7 fusion.106
  125.6 1.7 fusion.106
  128.1 1.7 fusion.106
  130.6 1.7 fusion.106
  133.0 1.7 fusion.106
  135.5 1.7 fusion.106
  137.2 1.3 convolution_convert_fusion.1
  138.5 6.6 %all_to_all.38 = bf16[2,12,48,128]{3,2,1,0:T(8,128)(2,1)S(1)} all-to-all(bf16[2,12,48,128]{3,2,1,0:T(8,128)(2,1)S(1)} %bitcast.194), channel_id=1, replica_groups=mesh['grp'=2,'row'=32,'col'=4,'sub'=2] {'sub'}, dimensions={0} | all-to-all | bytes 589824 | tf_op jit(solution)/shard_map/all_to_all | solution.py:52
  147.1 3.2 stack.2
  150.4 22.9 %all-to-all-start.3 = ((bf16[32,12,48,128]{3,2,1,0:T(8,128)(2,1)}), bf16[32,12,48,128]{3,2,1,0:T(8,128)(2,1)}, u32[]{:S(2)}, u32[]{:S(2)}) async-start(bf16[32,12,48,128]{3,2,1,0:T(8,128)(2,1)} %stack.2), calls=%async_computation.3 | async-start | bytes 9437184 | tf_op jit(solution)/shard_map/all_to_all | solution.py:11
  173.7 405.6 %all-to-all-done.3 = bf16[32,12,48,128]{3,2,1,0:T(8,128)(2,1)} async-done(((bf16[32,12,48,128]{3,2,1,0:T(8,128)(2,1)}), bf16[32,12,48,128]{3,2,1,0:T(8,128)(2,1)}, u32[]{:S(2)}, u32[]{:S(2)}) %all-to-all-start.3) | async-done | bytes 4718624 | tf_op jit(solution)/shard_map/all_to_all | solution.py:11
  579.3 7.6 %copy.81 = bf16[384,48,128]{0,1,2:T(8,128)(2,1)} copy(bf16[384,48,128]{2,1,0:T(8,128)(2,1)} %bitcast.37) | data formatting | bytes 9437184 | tf_op jit(solution)/shard_map/reshape | solution.py:10
  586.9 3.3 fusion.20
  592.6 4.5 all-to-all-start.4
  597.3 16.2 %all-to-all-done.4 = bf16[8,12,48,128]{3,2,1,0:T(8,128)(2,1)S(1)} async-done(((bf16[8,12,48,128]{3,2,1,0:T(8,128)(2,1)}), bf16[8,12,48,128]{3,2,1,0:T(8,128)(2,1)S(1)}, u32[]{:S(2)}, u32[]{:S(2)}) %all-to-all-start.4) | async-done | bytes 1179680 | tf_op jit(solution)/shard_map/all_to_all | solution.py:52
  (93 shorter events, 18.3 us)
Async XLA Ops:
  6.5 608.8 %copy-start = (bf16[512,128]{1,0:T(8,128)(2,1)S(1)}, bf16[512,128]{1,0:T(8,128)(2,1)}, u32[]{:S(2)}) copy-start(bf16[512,128]{1,0:T(8,128)(2,1)} %param.25) | copy-start | bytes 393220
  6.6 51.4 %copy-start.1 = (bf16[12,96,128]{2,1,0:T(8,128)(2,1)S(1)}, bf16[12,96,128]{2,1,0:T(8,128)(2,1)}, u32[]{:S(2)}) copy-start(bf16[12,96,128]{2,1,0:T(8,128)(2,1)} %param.14) | copy-start | bytes 884740
  6.6 51.4 %copy-start.6 = (bf16[128,4,64]{0,2,1:T(8,128)(2,1)S(1)}, bf16[128,4,64]{0,2,1:T(8,128)(2,1)}, u32[]{:S(2)}) copy-start(bf16[128,4,64]{0,2,1:T(8,128)(2,1)} %param.17) | copy-start | bytes 196612
  11.5 97.7 %all-to-all-start = ((f32[32,2,12,96]{3,1,2,0:T(2,128)}), f32[32,2,12,96]{3,1,2,0:T(2,128)}, u32[]{:S(2)}, u32[]{:S(2)}) async-start(f32[32,2,12,96]{3,1,2,0:T(2,128)} %broadcast_in_dim.8), calls=%async_computation | async-start | bytes 786432 | tf_op jit(solution)/shard_map/all_to_all | solution.py:36
  57.9 55.7 %all-gather.2.cloned.1.call-start = ((), (), s32[]{:S(2)}) async-start(), calls=%async_computation.5 | async-start | bytes 2949120 | tf_op jit(solution)/shard_map/all_gather | solution.py:25
  58.8 2.6 copy-start.2
  58.9 2.1 copy-start.5
  58.9 2.3 copy-start.8
  109.2 12.2 %all-to-all-start.1 = ((f32[2,384,96]{2,0,1:T(2,128)}), f32[2,384,96]{2,0,1:T(2,128)S(1)}, u32[]{:S(2)}, u32[]{:S(2)}) async-start(f32[2,384,96]{2,0,1:T(2,128)} %bitcast.19), calls=%async_computation.1 | async-start | bytes 786432 | tf_op jit(solution)/shard_map/all_to_all | solution.py:106
  119.9 2.0 copy-start.9
  121.4 1.0 copy-start.13
  122.4 14.8 %copy-start.12 = (bf16[64,128]{1,0:T(8,128)(2,1)S(1)}, bf16[64,128]{1,0:T(8,128)(2,1)}, u32[]{:S(2)}) copy-start(bf16[64,128]{1,0:T(8,128)(2,1)} %param.20) | copy-start | bytes 49156
  145.9 0.7 copy-start.3
  150.4 429.0 %all-to-all-start.3 = ((bf16[32,12,48,128]{3,2,1,0:T(8,128)(2,1)}), bf16[32,12,48,128]{3,2,1,0:T(8,128)(2,1)}, u32[]{:S(2)}, u32[]{:S(2)}) async-start(bf16[32,12,48,128]{3,2,1,0:T(8,128)(2,1)} %stack.2), calls=%async_computation.3 | async-start | bytes 9437184 | tf_op jit(solution)/shard_map/all_to_all | solution.py:11
  592.6 4.5 copy-start.4
  592.6 4.5 copy-start.11
  592.6 21.0 %all-to-all-start.4 = ((bf16[8,12,48,128]{3,2,1,0:T(8,128)(2,1)}), bf16[8,12,48,128]{3,2,1,0:T(8,128)(2,1)S(1)}, u32[]{:S(2)}, u32[]{:S(2)}) async-start(bf16[8,12,48,128]{3,2,1,0:T(8,128)(2,1)} %copy.84), calls=%async_computation.4 | async-start | bytes 2359296 | tf_op jit(solution)/shard_map/all_to_all | solution.py:52
  597.1 17.4 %copy-start.7 = (bf16[128,128]{1,0:T(8,128)(2,1)S(1)}, bf16[128,128]{1,0:T(8,128)(2,1)}, u32[]{:S(2)}) copy-start(bf16[128,128]{1,0:T(8,128)(2,1)} %param.23) | copy-start | bytes 98308
  614.1 1.2 copy-start.10
Sparse Core Ops, SparseCore 0:
  60.8 50.1 all-gather.1
